TPU v7x, 32 devices: a whole 2x2x4 slice. The times are simulated.
32 devices in a mesh: layer: 2 (over core), row: 4 (over y, x), col: 4 (over z).
Axes of the slice: x: 2, y: 2, z: 4, core: 2. Of those that a mesh axis runs over, the one named last changes fastest.
Arguments:
- root_rhs: float32 [32, 8, 1024], P(None, None, 'row'), may hold values from -6 to 6
- child_rhs: float32 [2, 32, 8, 1024], P('layer', None, None, 'row'), may hold values from -6 to 6
- root_factor: float32 [8, 8, 1024, 1024], P(None, None, 'row', 'col'), may hold values from -0.0625 to 0.0625
- child_factor: float32 [2, 8, 8, 1024, 1024], P('layer', None, None, 'row', 'col'), may hold values from -0.0625 to 0.0625
- coupling: float32 [2, 8, 8, 1024, 1024], P('layer', None, None, 'row', 'col'), may hold values from -0.0234375 to 0.0234375
- root_inverse: float32 [8, 1024, 1024], P(None, 'col', 'row'), as said below
- child_inverse: float32 [2, 8, 1024, 1024], P('layer', None, 'col', 'row'), as said below
Outputs:
- root_solution: float32 [32, 8, 1024], P(None, None, 'row')
- child_solution: float32 [2, 32, 8, 1024], P('layer', None, None, 'row')
Inputs may be any that keep to these rules, and one draw needn't show every extreme that they name: Each block of root_inverse is lower triangular. Each block of child_inverse is lower triangular.
All inputs are finite; a program needn't handle non-finite values.
Results may differ from a plain program's by a relative error of at most 0.00015.
Values sent between devices are 32-bit elements; how exact they have to be, the bound alone decides.
No kernel may reach another device: no remote copies, remote signals or barrier semaphores. Data moves between devices by JAX's collectives and lax.ppermute only.
A program may use at most 128 MiB of HBM per device.

v0:
```python
import jax
import jax.numpy as jnp
from jax import lax
from jax.sharding import PartitionSpec as P

precise = lax.Precision.HIGHEST


def pick(stack, index, axis):
    return lax.dynamic_index_in_dim(stack, index, axis, keepdims=False)


def forward(factor, inverse, right, extra, first_col):
    blocks = factor.shape[0]
    columns = right.shape[0]
    col_width = factor.shape[3]
    right_rows = jnp.transpose(right, (1, 0, 2))
    solved = jnp.zeros((blocks, columns, col_width), jnp.float32)

    def forward_step(target, solved):
        row_tiles = pick(factor, target, 0)
        partial_value = jnp.where(first_col, pick(right_rows, target, 0), 0.0) - pick(
            extra, target, 0
        )
        partial_value = partial_value - jnp.einsum(
            "jna,jba->nb", solved, row_tiles, precision=precise
        )
        residual = lax.psum(partial_value, "col")
        share = jnp.einsum("nb,ab->na", residual, pick(inverse, target, 0), precision=precise)
        solved_block = lax.psum(share, "row")
        return lax.dynamic_update_index_in_dim(solved, solved_block, target, 0)

    return lax.fori_loop(0, blocks, forward_step, solved)


def backward(factor, inverse, values, lowered, first_row):
    blocks = factor.shape[0]
    columns = values.shape[1]
    row_width = factor.shape[2]
    solved = jnp.zeros((blocks, columns, row_width), jnp.float32)

    def backward_step(step_at, solved):
        target = blocks - 1 - step_at
        column_tiles = pick(factor, target, 1)
        partial_value = jnp.where(first_row, pick(values, target, 0), 0.0) - pick(
            lowered, target, 0
        )
        partial_value = partial_value - jnp.einsum(
            "inb,iba->na", solved, column_tiles, precision=precise
        )
        pending = lax.psum(partial_value, "row")
        share = jnp.einsum("na,ab->nb", pending, pick(inverse, target, 0), precision=precise)
        solved_block = lax.psum(share, "col")
        return lax.dynamic_update_index_in_dim(solved, solved_block, target, 0)

    return lax.fori_loop(0, blocks, backward_step, solved)


def local(root_rhs, child_rhs, root_factor, child_factor, coupling, root_inverse, child_inverse):
    first_row = lax.axis_index("row") == 0
    first_col = lax.axis_index("col") == 0
    columns = root_rhs.shape[0]
    child_blocks = child_factor[0]
    child_inverses = child_inverse[0]
    couple_blocks = coupling[0]
    child_count = child_blocks.shape[0]
    root_count = root_factor.shape[0]
    row_width = root_factor.shape[2]
    col_width = root_factor.shape[3]
    child_down, root_down = (child_inverses, root_inverse)
    child_up, root_up = (child_inverses, root_inverse)
    child_start = jnp.zeros((child_count, columns, row_width), jnp.float32)
    child_forward = forward(child_blocks, child_down, child_rhs[0], child_start, first_col)
    lifted = jnp.einsum("jna,kjba->knb", child_forward, couple_blocks, precision=precise)
    lifted = lax.psum_scatter(lifted, "layer", scatter_dimension=1, tiled=True)
    half_cols = lifted.shape[1]
    layer_index = lax.axis_index("layer")
    right_half = lax.dynamic_slice_in_dim(root_rhs, layer_index * half_cols, half_cols, 0)
    root_forward = forward(root_factor, root_down, right_half, lifted, first_col)
    empty = jnp.zeros((root_count, half_cols, col_width), jnp.float32)
    root_half = backward(root_factor, root_up, root_forward, empty, first_row)
    root_solved = lax.all_gather(root_half, "layer", axis=1, tiled=True)
    lowered = jnp.einsum("inb,ikba->kna", root_solved, couple_blocks, precision=precise)
    child_solved = backward(child_blocks, child_up, child_forward, lowered, first_row)
    root_solution = jnp.transpose(root_solved, (1, 0, 2))
    child_solution = jnp.transpose(child_solved, (1, 0, 2))[None]
    return (root_solution, child_solution)


def solution(mesh):
    in_specs = (
        P(None, None, "row"),
        P("layer", None, None, "row"),
        P(None, None, "row", "col"),
        P("layer", None, None, "row", "col"),
        P("layer", None, None, "row", "col"),
        P(None, "col", "row"),
        P("layer", None, "col", "row"),
    )
    out_specs = (P(None, None, "row"), P("layer", None, None, "row"))
    return jax.shard_map(local, mesh=mesh, in_specs=in_specs, out_specs=out_specs, check_vma=False)
```

profile of v0, /device:TPU:0, one launch (start us, length us, event | category | flops | bytes accessed | tf_op | source)
XLA Modules:
  0.0 1199.0 jit_solution(10742382642102309621)
XLA Ops:
  8.3 295.6 %while.56 = (s32[]{:T(128)}, f32[8,32,256]{2,1,0:T(8,128)S(1)}, pred[]{:T(512)}, f32[8,32,256]{2,1,0:T(8,128)S(1)}, f32[8,8,256,256]{3,2,1,0:T(8,128)}, /*index=5*/f32[8,256,256]{2,1,0:T(8,128)}, s32[]{:T(128)}) while((s32[]{:T(128)}, f32[8,32,256]{2,1,0:T(8,128)S(1)}, pred[]{:T(512)}, f32[8,32,256]{2,1,0:T(8,128)S(1)}, ...), condition=%wide.region_3.4_spmd, body=%wide.region_0.3_spmd.sunk | while | flops 226525184 | bytes 2950749 | solution.py:33
  11.8 20.9 %psum.108 = f32[32,256]{1,0:T(8,128)S(1)} all-reduce(f32[32,256]{1,0:T(8,128)S(1)} %fusion.96), channel_id=1, replica_groups=mesh['layer'=2,'row'=4,'col'=4] {'col'}, use_global_device_ids=true, to_apply=%region_1.1 | all-reduce | flops 8192 | bytes 65536 | tf_op jit(solution)/shard_map/while/body/eval_jaxpr/psum | solution.py:28
  34.0 16.3 %psum.109 = f32[1,32,256]{2,1,0:T(8,128)S(1)} all-reduce(f32[1,32,256]{2,1,0:T(8,128)S(1)} %convolution_bitcast_fusion.8), channel_id=1, replica_groups=mesh['layer'=2,'row'=4,'col'=4] {'row'}, use_global_device_ids=true, to_apply=%region_2.2 | all-reduce | flops 8192 | bytes 65536 | tf_op jit(solution)/shard_map/while/body/eval_jaxpr/psum | solution.py:30
  88.6 17.5 %psum.108 = f32[32,256]{1,0:T(8,128)S(1)} all-reduce(f32[32,256]{1,0:T(8,128)S(1)} %fusion.96), channel_id=1, replica_groups=mesh['layer'=2,'row'=4,'col'=4] {'col'}, use_global_device_ids=true, to_apply=%region_1.1 | all-reduce | flops 8192 | bytes 65536 | tf_op jit(solution)/shard_map/while/body/eval_jaxpr/psum | solution.py:28
  161.3 17.5 %psum.108 = f32[32,256]{1,0:T(8,128)S(1)} all-reduce(f32[32,256]{1,0:T(8,128)S(1)} %fusion.96), channel_id=1, replica_groups=mesh['layer'=2,'row'=4,'col'=4] {'col'}, use_global_device_ids=true, to_apply=%region_1.1 | all-reduce | flops 8192 | bytes 65536 | tf_op jit(solution)/shard_map/while/body/eval_jaxpr/psum | solution.py:28
  180.1 16.3 %psum.109 = f32[1,32,256]{2,1,0:T(8,128)S(1)} all-reduce(f32[1,32,256]{2,1,0:T(8,128)S(1)} %convolution_bitcast_fusion.8), channel_id=1, replica_groups=mesh['layer'=2,'row'=4,'col'=4] {'row'}, use_global_device_ids=true, to_apply=%region_2.2 | all-reduce | flops 8192 | bytes 65536 | tf_op jit(solution)/shard_map/while/body/eval_jaxpr/psum | solution.py:30
  234.8 17.4 %psum.108 = f32[32,256]{1,0:T(8,128)S(1)} all-reduce(f32[32,256]{1,0:T(8,128)S(1)} %fusion.96), channel_id=1, replica_groups=mesh['layer'=2,'row'=4,'col'=4] {'col'}, use_global_device_ids=true, to_apply=%region_1.1 | all-reduce | flops 8192 | bytes 65536 | tf_op jit(solution)/shard_map/while/body/eval_jaxpr/psum | solution.py:28
  303.9 19.2 %fusion.56 = f32[8,32,256]{2,1,0:T(8,128)} fusion(f32[1,8,8,256,256]{4,3,2,1,0:T(8,128)} %param.19, f32[8,32,256]{2,1,0:T(8,128)S(1)} %get-tuple-element.861), kind=kOutput, calls=%fused_computation.48 | convolution fusion | flops 1610612736 | bytes 17301504 | tf_op jit(solution)/shard_map/jna,kjba->knb/dot_general | solution.py:74
  330.4 284.1 %while.57 = (s32[]{:T(128)}, f32[8,16,256]{2,1,0:T(8,128)S(1)}, pred[]{:T(512)}, f32[8,16,256]{2,1,0:T(8,128)S(1)}, f32[8,16,256]{2,1,0:T(8,128)}, /*index=5*/f3...) while((s32[]{:T(128)}, f32[8,16,256]{2,1,0:T(8,128)S(1)}, pred[]{:T(512)}, ...), condition=%wide.region_8.9_spmd, body=%wide.region_5.8_spmd.sunk | while | flops 113266688 | bytes 2672229 | solution.py:33
  333.7 18.9 %psum.110 = f32[16,256]{1,0:T(8,128)S(1)} all-reduce(f32[16,256]{1,0:T(8,128)S(1)} %fusion.101), channel_id=1, replica_groups=mesh['layer'=2,'row'=4,'col'=4] {'col'}, use_global_device_ids=true, to_apply=%region_6.6 | all-reduce | flops 4096 | bytes 32768 | tf_op jit(solution)/shard_map/while/body/eval_jaxpr/psum | solution.py:28
  407.2 16.3 %psum.110 = f32[16,256]{1,0:T(8,128)S(1)} all-reduce(f32[16,256]{1,0:T(8,128)S(1)} %fusion.101), channel_id=1, replica_groups=mesh['layer'=2,'row'=4,'col'=4] {'col'}, use_global_device_ids=true, to_apply=%region_6.6 | all-reduce | flops 4096 | bytes 32768 | tf_op jit(solution)/shard_map/while/body/eval_jaxpr/psum | solution.py:28
  477.4 16.3 %psum.110 = f32[16,256]{1,0:T(8,128)S(1)} all-reduce(f32[16,256]{1,0:T(8,128)S(1)} %fusion.101), channel_id=1, replica_groups=mesh['layer'=2,'row'=4,'col'=4] {'col'}, use_global_device_ids=true, to_apply=%region_6.6 | all-reduce | flops 4096 | bytes 32768 | tf_op jit(solution)/shard_map/while/body/eval_jaxpr/psum | solution.py:28
  614.5 274.9 %while.58 = (s32[]{:T(128)}, f32[8,16,256]{2,1,0:T(8,128)S(1)}, pred[]{:T(512)}, f32[8,16,256]{2,1,0:T(8,128)S(1)}, f32[8,8,256,256]{3,2,1,0:T(8,128)}, /*index=...) while((s32[]{:T(128)}, f32[8,16,256]{2,1,0:T(8,128)S(1)}, pred[]{:T(512)}, ...), condition=%wide.region_12.13_spmd, body=%wide.region_9.12_spmd.sunk | while | flops 113262600 | bytes 2655907 | solution.py:56
  771.2 16.3 %psum.113 = f32[1,16,256]{2,1,0:T(8,128)S(1)} all-reduce(f32[1,16,256]{2,1,0:T(8,128)S(1)} %convolution_bitcast_fusion.10), channel_id=1, replica_groups=mesh['layer'=2,'row'=4,'col'=4] {'col'}, use_global_device_ids=true, to_apply=%region_11.11 | all-reduce | flops 4096 | bytes 32768 | tf_op jit(solution)/shard_map/while/body/eval_jaxpr/psum | solution.py:53
  839.9 16.3 %psum.113 = f32[1,16,256]{2,1,0:T(8,128)S(1)} all-reduce(f32[1,16,256]{2,1,0:T(8,128)S(1)} %convolution_bitcast_fusion.10), channel_id=1, replica_groups=mesh['layer'=2,'row'=4,'col'=4] {'col'}, use_global_device_ids=true, to_apply=%region_11.11 | all-reduce | flops 4096 | bytes 32768 | tf_op jit(solution)/shard_map/while/body/eval_jaxpr/psum | solution.py:53
  905.6 285.7 %while.59 = (s32[]{:T(128)}, f32[8,32,256]{2,1,0:T(8,128)S(1)}, pred[]{:T(512)}, f32[8,32,256]{2,1,0:T(8,128)S(1)}, f32[8,32,256]{2,1,0:T(8,128)S(1)}, /*index=5...) while((s32[]{:T(128)}, f32[8,32,256]{2,1,0:T(8,128)S(1)}, ...), condition=%wide.region_16.17_spmd, body=%wide.region_13.16_spmd.sunk | while | flops 226533376 | bytes 2983595 | solution.py:56
  925.2 16.6 %psum.115 = f32[1,32,256]{2,1,0:T(8,128)S(1)} all-reduce(f32[1,32,256]{2,1,0:T(8,128)S(1)} %convolution_bitcast_fusion.11), channel_id=1, replica_groups=mesh['layer'=2,'row'=4,'col'=4] {'col'}, use_global_device_ids=true, to_apply=%region_15.15 | all-reduce | flops 8192 | bytes 65536 | tf_op jit(solution)/shard_map/while/body/eval_jaxpr/psum | solution.py:53
  960.0 16.7 %psum.115 = f32[1,32,256]{2,1,0:T(8,128)S(1)} all-reduce(f32[1,32,256]{2,1,0:T(8,128)S(1)} %convolution_bitcast_fusion.11), channel_id=1, replica_groups=mesh['layer'=2,'row'=4,'col'=4] {'col'}, use_global_device_ids=true, to_apply=%region_15.15 | all-reduce | flops 8192 | bytes 65536 | tf_op jit(solution)/shard_map/while/body/eval_jaxpr/psum | solution.py:53
  996.2 16.6 %psum.115 = f32[1,32,256]{2,1,0:T(8,128)S(1)} all-reduce(f32[1,32,256]{2,1,0:T(8,128)S(1)} %convolution_bitcast_fusion.11), channel_id=1, replica_groups=mesh['layer'=2,'row'=4,'col'=4] {'col'}, use_global_device_ids=true, to_apply=%region_15.15 | all-reduce | flops 8192 | bytes 65536 | tf_op jit(solution)/shard_map/while/body/eval_jaxpr/psum | solution.py:53
  1031.6 16.9 %psum.115 = f32[1,32,256]{2,1,0:T(8,128)S(1)} all-reduce(f32[1,32,256]{2,1,0:T(8,128)S(1)} %convolution_bitcast_fusion.11), channel_id=1, replica_groups=mesh['layer'=2,'row'=4,'col'=4] {'col'}, use_global_device_ids=true, to_apply=%region_15.15 | all-reduce | flops 8192 | bytes 65536 | tf_op jit(solution)/shard_map/while/body/eval_jaxpr/psum | solution.py:53
  1068.0 16.7 %psum.115 = f32[1,32,256]{2,1,0:T(8,128)S(1)} all-reduce(f32[1,32,256]{2,1,0:T(8,128)S(1)} %convolution_bitcast_fusion.11), channel_id=1, replica_groups=mesh['layer'=2,'row'=4,'col'=4] {'col'}, use_global_device_ids=true, to_apply=%region_15.15 | all-reduce | flops 8192 | bytes 65536 | tf_op jit(solution)/shard_map/while/body/eval_jaxpr/psum | solution.py:53
  1103.0 16.7 %psum.115 = f32[1,32,256]{2,1,0:T(8,128)S(1)} all-reduce(f32[1,32,256]{2,1,0:T(8,128)S(1)} %convolution_bitcast_fusion.11), channel_id=1, replica_groups=mesh['layer'=2,'row'=4,'col'=4] {'col'}, use_global_device_ids=true, to_apply=%region_15.15 | all-reduce | flops 8192 | bytes 65536 | tf_op jit(solution)/shard_map/while/body/eval_jaxpr/psum | solution.py:53
  1139.1 16.6 %psum.115 = f32[1,32,256]{2,1,0:T(8,128)S(1)} all-reduce(f32[1,32,256]{2,1,0:T(8,128)S(1)} %convolution_bitcast_fusion.11), channel_id=1, replica_groups=mesh['layer'=2,'row'=4,'col'=4] {'col'}, use_global_device_ids=true, to_apply=%region_15.15 | all-reduce | flops 8192 | bytes 65536 | tf_op jit(solution)/shard_map/while/body/eval_jaxpr/psum | solution.py:53
  1174.3 16.9 %psum.115 = f32[1,32,256]{2,1,0:T(8,128)S(1)} all-reduce(f32[1,32,256]{2,1,0:T(8,128)S(1)} %convolution_bitcast_fusion.11), channel_id=1, replica_groups=mesh['layer'=2,'row'=4,'col'=4] {'col'}, use_global_device_ids=true, to_apply=%region_15.15 | all-reduce | flops 8192 | bytes 65536 | tf_op jit(solution)/shard_map/while/body/eval_jaxpr/psum | solution.py:53
  (157 shorter events, 840.7 us)
Async XLA Ops:
  7.2 316.0 %copy-start = (f32[32,8,256]{2,1,0:T(8,128)S(1)}, f32[32,8,256]{2,1,0:T(8,128)}, u32[]{:S(2)}) copy-start(f32[32,8,256]{2,1,0:T(8,128)} %param.15) | copy-start | bytes 786436
  7.2 323.2 %reduce-scatter.2.cloned.1.call-start = ((), (), s32[]{:S(2)}) async-start(), calls=%async_computation.1 | async-start | bytes 393216 | tf_op jit(solution)/shard_map/reduce_scatter | solution.py:75
Sparse Core Ops, SparseCore 0:
  323.2 7.0 reduce-scatter.1
where the time goes:
time: 1200 us
  blocking collectives  1000 us (83%)
  matrix products  169 us (14%)
  between operations  14.1 us (1%)
    psum x16, blocking collectives, forward_step(): residual = lax.psum(partial_value, 'col')  266 us
    psum x16, blocking collectives, backward_step(): solved_block = lax.psum(share, 'col')  261 us
    psum x16, blocking collectives, forward_step(): solved_block = lax.psum(share, 'row')  238 us
    psum x16, blocking collectives, backward_step(): pending = lax.psum(partial_value, 'row')  236 us
    dot_general x16, matrix products, forward_step(): jnp.einsum('jna,jba->nb', solved, row_tiles, precision=precise)  54.5 us
    dot_general x16, matrix products, backward_step(): jnp.einsum('inb,iba->na', solved, column_tiles, precision=precise)  43.7 us
  transfers between devices with their start and end apart: 1, of which 1 were waited for; matrix products, arithmetic and copies ran while one was open for 0% of the time, Pallas kernels for 0%

commit v1 on v0

--- a/solution.py
+++ b/solution.py
@@ -50,7 +50,11 @@
         )
         pending = lax.psum(partial_value, "row")
         share = jnp.einsum("na,ab->nb", pending, pick(inverse, target, 0), precision=precise)
-        solved_block = lax.psum(share, "col")
+        solved_block = share
+        for hop in (1, 2):
+            solved_block = solved_block + lax.ppermute(
+                solved_block, "col", [(dev, dev ^ hop) for dev in range(4)]
+            )
         return lax.dynamic_update_index_in_dim(solved, solved_block, target, 0)
 
     return lax.fori_loop(0, blocks, backward_step, solved)

time: 1200 us -> 1080 us (0.900)
  blocking collectives: 1000 us -> 743 us
  waiting for transfers between devices: 7.17 us -> 140 us
    psum x16 -> x0, blocking collectives: 261 us -> none  [backward_step(): solved_block = lax.psum(share, 'col')]
    ppermute x0 -> x32, waiting for transfers between devices: none -> 132 us  [backward_step(): lax.ppermute(solved_block, 'col', [(dev, dev ^ hop) for dev in range(4)])]
  transfers between devices with their start and end apart: 1 -> 33, of which waited for: 1 -> 33; matrix products, arithmetic and copies ran while one was open for 0% -> 0% of each run, Pallas kernels for 0% -> 0%
where the time goes in v1:
time: 1080 us
  blocking collectives  743 us (69%)
  matrix products  169 us (16%)
  waiting for transfers between devices  140 us (13%)
  between operations  14.1 us (1%)
    psum x16, blocking collectives, forward_step(): residual = lax.psum(partial_value, 'col')  266 us
    psum x16, blocking collectives, forward_step(): solved_block = lax.psum(share, 'row')  238 us
    psum x16, blocking collectives, backward_step(): pending = lax.psum(partial_value, 'row')  237 us
    ppermute x32, waiting for transfers between devices, backward_step(): lax.ppermute(solved_block, 'col', [(dev, dev ^ hop) for dev in range(4)])  132 us
    dot_general x16, matrix products, forward_step(): jnp.einsum('jna,jba->nb', solved, row_tiles, precision=precise)  54.5 us
    dot_general x16, matrix products, backward_step(): jnp.einsum('inb,iba->na', solved, column_tiles, precision=precise)  43.7 us
  transfers between devices with their start and end apart: 33, of which 33 were waited for; matrix products, arithmetic and copies ran while one was open for 0% of the time, Pallas kernels for 0%

profile of v1, /device:TPU:0, one launch (start us, length us, event | category | flops | bytes accessed | tf_op | source)
XLA Modules:
  0.0 1076.1 jit_solution(8900188943634942839)
XLA Ops:
  8.3 295.6 %while.56 = (s32[]{:T(128)}, f32[8,32,256]{2,1,0:T(8,128)S(1)}, pred[]{:T(512)}, f32[8,32,256]{2,1,0:T(8,128)S(1)}, f32[8,8,256,256]{3,2,1,0:T(8,128)}, /*index=5*/f32[8,256,256]{2,1,0:T(8,128)}, s32[]{:T(128)}) while((s32[]{:T(128)}, f32[8,32,256]{2,1,0:T(8,128)S(1)}, pred[]{:T(512)}, f32[8,32,256]{2,1,0:T(8,128)S(1)}, ...), condition=%wide.region_3.4_spmd, body=%wide.region_0.3_spmd.sunk | while | flops 226525184 | bytes 2950749 | solution.py:33
  11.8 20.9 %psum.78 = f32[32,256]{1,0:T(8,128)S(1)} all-reduce(f32[32,256]{1,0:T(8,128)S(1)} %fusion.100), channel_id=1, replica_groups=mesh['layer'=2,'row'=4,'col'=4] {'col'}, use_global_device_ids=true, to_apply=%region_1.1 | all-reduce | flops 8192 | bytes 65536 | tf_op jit(solution)/shard_map/while/body/eval_jaxpr/psum | solution.py:28
  34.0 16.3 %psum.79 = f32[1,32,256]{2,1,0:T(8,128)S(1)} all-reduce(f32[1,32,256]{2,1,0:T(8,128)S(1)} %convolution_bitcast_fusion.4), channel_id=1, replica_groups=mesh['layer'=2,'row'=4,'col'=4] {'row'}, use_global_device_ids=true, to_apply=%region_2.2 | all-reduce | flops 8192 | bytes 65536 | tf_op jit(solution)/shard_map/while/body/eval_jaxpr/psum | solution.py:30
  53.8 15.8 %psum.78 = f32[32,256]{1,0:T(8,128)S(1)} all-reduce(f32[32,256]{1,0:T(8,128)S(1)} %fusion.100), channel_id=1, replica_groups=mesh['layer'=2,'row'=4,'col'=4] {'col'}, use_global_device_ids=true, to_apply=%region_1.1 | all-reduce | flops 8192 | bytes 65536 | tf_op jit(solution)/shard_map/while/body/eval_jaxpr/psum | solution.py:28
  88.6 17.5 %psum.78 = f32[32,256]{1,0:T(8,128)S(1)} all-reduce(f32[32,256]{1,0:T(8,128)S(1)} %fusion.100), channel_id=1, replica_groups=mesh['layer'=2,'row'=4,'col'=4] {'col'}, use_global_device_ids=true, to_apply=%region_1.1 | all-reduce | flops 8192 | bytes 65536 | tf_op jit(solution)/shard_map/while/body/eval_jaxpr/psum | solution.py:28
  107.5 15.6 %psum.79 = f32[1,32,256]{2,1,0:T(8,128)S(1)} all-reduce(f32[1,32,256]{2,1,0:T(8,128)S(1)} %convolution_bitcast_fusion.4), channel_id=1, replica_groups=mesh['layer'=2,'row'=4,'col'=4] {'row'}, use_global_device_ids=true, to_apply=%region_2.2 | all-reduce | flops 8192 | bytes 65536 | tf_op jit(solution)/shard_map/while/body/eval_jaxpr/psum | solution.py:30
  126.5 15.8 %psum.78 = f32[32,256]{1,0:T(8,128)S(1)} all-reduce(f32[32,256]{1,0:T(8,128)S(1)} %fusion.100), channel_id=1, replica_groups=mesh['layer'=2,'row'=4,'col'=4] {'col'}, use_global_device_ids=true, to_apply=%region_1.1 | all-reduce | flops 8192 | bytes 65536 | tf_op jit(solution)/shard_map/while/body/eval_jaxpr/psum | solution.py:28
  161.3 17.5 %psum.78 = f32[32,256]{1,0:T(8,128)S(1)} all-reduce(f32[32,256]{1,0:T(8,128)S(1)} %fusion.100), channel_id=1, replica_groups=mesh['layer'=2,'row'=4,'col'=4] {'col'}, use_global_device_ids=true, to_apply=%region_1.1 | all-reduce | flops 8192 | bytes 65536 | tf_op jit(solution)/shard_map/while/body/eval_jaxpr/psum | solution.py:28
  180.1 16.3 %psum.79 = f32[1,32,256]{2,1,0:T(8,128)S(1)} all-reduce(f32[1,32,256]{2,1,0:T(8,128)S(1)} %convolution_bitcast_fusion.4), channel_id=1, replica_groups=mesh['layer'=2,'row'=4,'col'=4] {'row'}, use_global_device_ids=true, to_apply=%region_2.2 | all-reduce | flops 8192 | bytes 65536 | tf_op jit(solution)/shard_map/while/body/eval_jaxpr/psum | solution.py:30
  199.9 15.8 %psum.78 = f32[32,256]{1,0:T(8,128)S(1)} all-reduce(f32[32,256]{1,0:T(8,128)S(1)} %fusion.100), channel_id=1, replica_groups=mesh['layer'=2,'row'=4,'col'=4] {'col'}, use_global_device_ids=true, to_apply=%region_1.1 | all-reduce | flops 8192 | bytes 65536 | tf_op jit(solution)/shard_map/while/body/eval_jaxpr/psum | solution.py:28
  234.8 17.4 %psum.78 = f32[32,256]{1,0:T(8,128)S(1)} all-reduce(f32[32,256]{1,0:T(8,128)S(1)} %fusion.100), channel_id=1, replica_groups=mesh['layer'=2,'row'=4,'col'=4] {'col'}, use_global_device_ids=true, to_apply=%region_1.1 | all-reduce | flops 8192 | bytes 65536 | tf_op jit(solution)/shard_map/while/body/eval_jaxpr/psum | solution.py:28
  272.6 15.8 %psum.78 = f32[32,256]{1,0:T(8,128)S(1)} all-reduce(f32[32,256]{1,0:T(8,128)S(1)} %fusion.100), channel_id=1, replica_groups=mesh['layer'=2,'row'=4,'col'=4] {'col'}, use_global_device_ids=true, to_apply=%region_1.1 | all-reduce | flops 8192 | bytes 65536 | tf_op jit(solution)/shard_map/while/body/eval_jaxpr/psum | solution.py:28
  303.9 19.2 %fusion.58 = f32[8,32,256]{2,1,0:T(8,128)} fusion(f32[1,8,8,256,256]{4,3,2,1,0:T(8,128)} %param.19, f32[8,32,256]{2,1,0:T(8,128)S(1)} %get-tuple-element.861), kind=kOutput, calls=%fused_computation.48 | convolution fusion | flops 1610612736 | bytes 17301504 | tf_op jit(solution)/shard_map/jna,kjba->knb/dot_general | solution.py:78
  330.4 284.1 %while.57 = (s32[]{:T(128)}, f32[8,16,256]{2,1,0:T(8,128)S(1)}, pred[]{:T(512)}, f32[8,16,256]{2,1,0:T(8,128)S(1)}, f32[8,16,256]{2,1,0:T(8,128)}, /*index=5*/f3...) while((s32[]{:T(128)}, f32[8,16,256]{2,1,0:T(8,128)S(1)}, pred[]{:T(512)}, ...), condition=%wide.region_8.9_spmd, body=%wide.region_5.8_spmd.sunk | while | flops 113266688 | bytes 2672229 | solution.py:33
  333.7 18.9 %psum.80 = f32[16,256]{1,0:T(8,128)S(1)} all-reduce(f32[16,256]{1,0:T(8,128)S(1)} %fusion.105), channel_id=1, replica_groups=mesh['layer'=2,'row'=4,'col'=4] {'col'}, use_global_device_ids=true, to_apply=%region_6.6 | all-reduce | flops 4096 | bytes 32768 | tf_op jit(solution)/shard_map/while/body/eval_jaxpr/psum | solution.py:28
  353.9 16.1 %psum.81 = f32[1,16,256]{2,1,0:T(8,128)S(1)} all-reduce(f32[1,16,256]{2,1,0:T(8,128)S(1)} %convolution_bitcast_fusion.5), channel_id=1, replica_groups=mesh['layer'=2,'row'=4,'col'=4] {'row'}, use_global_device_ids=true, to_apply=%region_7.7 | all-reduce | flops 4096 | bytes 32768 | tf_op jit(solution)/shard_map/while/body/eval_jaxpr/psum | solution.py:30
  407.2 16.3 %psum.80 = f32[16,256]{1,0:T(8,128)S(1)} all-reduce(f32[16,256]{1,0:T(8,128)S(1)} %fusion.105), channel_id=1, replica_groups=mesh['layer'=2,'row'=4,'col'=4] {'col'}, use_global_device_ids=true, to_apply=%region_6.6 | all-reduce | flops 4096 | bytes 32768 | tf_op jit(solution)/shard_map/while/body/eval_jaxpr/psum | solution.py:28
  477.4 16.3 %psum.80 = f32[16,256]{1,0:T(8,128)S(1)} all-reduce(f32[16,256]{1,0:T(8,128)S(1)} %fusion.105), channel_id=1, replica_groups=mesh['layer'=2,'row'=4,'col'=4] {'col'}, use_global_device_ids=true, to_apply=%region_6.6 | all-reduce | flops 4096 | bytes 32768 | tf_op jit(solution)/shard_map/while/body/eval_jaxpr/psum | solution.py:28
  547.6 16.3 %psum.80 = f32[16,256]{1,0:T(8,128)S(1)} all-reduce(f32[16,256]{1,0:T(8,128)S(1)} %fusion.105), channel_id=1, replica_groups=mesh['layer'=2,'row'=4,'col'=4] {'col'}, use_global_device_ids=true, to_apply=%region_6.6 | all-reduce | flops 4096 | bytes 32768 | tf_op jit(solution)/shard_map/while/body/eval_jaxpr/psum | solution.py:28
  583.9 15.6 %psum.80 = f32[16,256]{1,0:T(8,128)S(1)} all-reduce(f32[16,256]{1,0:T(8,128)S(1)} %fusion.105), channel_id=1, replica_groups=mesh['layer'=2,'row'=4,'col'=4] {'col'}, use_global_device_ids=true, to_apply=%region_6.6 | all-reduce | flops 4096 | bytes 32768 | tf_op jit(solution)/shard_map/while/body/eval_jaxpr/psum | solution.py:28
  614.5 215.2 %while.58 = (s32[]{:T(128)}, f32[8,16,256]{2,1,0:T(8,128)S(1)}, pred[]{:T(512)}, f32[8,16,256]{2,1,0:T(8,128)S(1)}, f32[8,8,256,256]{3,2,1,0:T(8,128)}, /*index=...) while((s32[]{:T(128)}, f32[8,16,256]{2,1,0:T(8,128)S(1)}, pred[]{:T(512)}, ...), condition=%wide.region_11.12_spmd, body=%wide.region_9.11_spmd.sunk | while | flops 113266696 | bytes 2819819 | solution.py:60
  845.8 222.6 %while.59 = (s32[]{:T(128)}, f32[8,32,256]{2,1,0:T(8,128)S(1)}, pred[]{:T(512)}, f32[8,32,256]{2,1,0:T(8,128)S(1)}, f32[8,32,256]{2,1,0:T(8,128)S(1)}, /*index=5...) while((s32[]{:T(128)}, f32[8,32,256]{2,1,0:T(8,128)S(1)}, ...), condition=%wide.region_14.15_spmd, body=%wide.region_12.14_spmd.sunk | while | flops 226541568 | bytes 3311347 | solution.py:60
  848.6 15.6 %psum.83 = f32[32,256]{1,0:T(8,128)S(1)} all-reduce(f32[32,256]{1,0:T(8,128)S(1)} %fusion.116), channel_id=1, replica_groups=mesh['layer'=2,'row'=4,'col'=4] {'row'}, use_global_device_ids=true, to_apply=%region_13.13 | all-reduce | flops 8192 | bytes 65536 | tf_op jit(solution)/shard_map/while/body/eval_jaxpr/psum | solution.py:51
  959.9 15.7 %psum.83 = f32[32,256]{1,0:T(8,128)S(1)} all-reduce(f32[32,256]{1,0:T(8,128)S(1)} %fusion.116), channel_id=1, replica_groups=mesh['layer'=2,'row'=4,'col'=4] {'row'}, use_global_device_ids=true, to_apply=%region_13.13 | all-reduce | flops 8192 | bytes 65536 | tf_op jit(solution)/shard_map/while/body/eval_jaxpr/psum | solution.py:51
  (221 shorter events, 726.4 us)
Async XLA Ops:
  7.2 323.2 %reduce-scatter.2.cloned.1.call-start = ((), (), s32[]{:S(2)}) async-start(), calls=%async_computation.1 | async-start | bytes 393216 | tf_op jit(solution)/shard_map/reduce_scatter | solution.py:79
  637.6 4.6 collective-permute-start.1
  663.7 4.6 collective-permute-start.1
  691.4 4.6 collective-permute-start.1
  717.5 4.6 collective-permute-start.1
  745.1 4.6 collective-permute-start.1
  771.2 4.6 collective-permute-start.1
  798.9 4.6 collective-permute-start.1
  825.0 4.6 collective-permute-start.1
  865.5 4.0 collective-permute-start.2
  869.4 4.8 collective-permute-start.3
  892.4 4.0 collective-permute-start.2
  896.4 4.8 collective-permute-start.3
  920.7 4.0 collective-permute-start.2
  924.7 4.8 collective-permute-start.3
  948.3 4.0 collective-permute-start.2
  952.3 4.8 collective-permute-start.3
  976.8 4.0 collective-permute-start.2
  980.8 4.8 collective-permute-start.3
  1004.0 4.0 collective-permute-start.2
  1008.0 4.8 collective-permute-start.3
  1032.1 4.0 collective-permute-start.2
  1036.1 4.8 collective-permute-start.3
  1063.6 4.8 collective-permute-start.3
  (10 other events, 350.4 us)
Sparse Core Ops, SparseCore 0:
  323.2 7.0 reduce-scatter.1
